TPU v7x, 32 devices: a whole 2x2x4 slice. The times are simulated.
32 devices in a mesh: gx: 2 (over core), gy: 4 (over y, x), gz: 4 (over z).
Axes of the slice: x: 2, y: 2, z: 4, core: 2. Of those that a mesh axis runs over, the one named last changes fastest.
Arguments:
- raw_weight: float32 [128, 27, 128], P(('gx', 'gy')), may hold values from -6 to 6
- inputs: bfloat16 [16, 64, 64, 128], P('gx', 'gy', 'gz'), may hold values from -6 to 6
- cotangent: bfloat16 [16, 64, 64, 128], P('gx', 'gy', 'gz'), may hold values from -0.099609375 to 0.099609375
Outputs:
- input_grad: bfloat16 [16, 64, 64, 128], P('gx', 'gy', 'gz')
- weight_grad: float32 [128, 27, 128], P(('gx', 'gy'))
All inputs are finite; a program needn't handle non-finite values.
Results may differ from a plain program's by a relative error of at most 0.0049.
Values may be sent and summed in bfloat16 or wider, within the bound.
A program may use at most 64 MiB of HBM per device.

v0:
```python
import jax
import jax.numpy as jnp
from jax import lax
from jax.sharding import PartitionSpec as P

var_eps = 1e-05
norm_eps = 1e-06
clip_norm = 600.0


def with_halo(cells, sides, width):
    for axis, dim in sides:
        count = lax.axis_size(axis)
        ends = count - 1
        head = lax.slice_in_dim(cells, 0, width, axis=dim)
        tail = lax.slice_in_dim(cells, cells.shape[dim] - width, cells.shape[dim], axis=dim)
        cells = jnp.concatenate(
            [
                lax.ppermute(tail, axis, [(i, (i + 1) % count) for i in range(ends)]),
                cells,
                lax.ppermute(head, axis, [((i + 1) % count, i) for i in range(ends)]),
            ],
            axis=dim,
        )
    return cells


def tap_view(padded, tap_a, tap_b, tap_c, extent):
    view = padded[
        2 - tap_a : 2 - tap_a + extent[0],
        2 - tap_b : 2 - tap_b + extent[1],
        2 - tap_c : 2 - tap_c + extent[2],
        :,
    ]
    return view.reshape(-1, view.shape[-1])


def input_rows(padded, extent, block_rows):
    row_count = block_rows.shape[0]
    total = jnp.zeros((extent[0] * extent[1] * extent[2], row_count), jnp.float32)
    for tap_a in range(3):
        for tap_b in range(3):
            for tap_c in range(3):
                tap_index = tap_a * 9 + tap_b * 3 + tap_c
                view = tap_view(padded, tap_a, tap_b, tap_c, extent)
                total = total + lax.dot_general(
                    view,
                    block_rows[:, tap_index, :],
                    (((1,), (1,)), ((), ())),
                    preferred_element_type=jnp.float32,
                )
    return total.astype(jnp.bfloat16).reshape(extent[0], extent[1], extent[2], row_count)


def filter_terms(padded, flat_in, extent):
    pieces = []
    for tap_a in range(3):
        for tap_b in range(3):
            for tap_c in range(3):
                view = tap_view(padded, tap_a, tap_b, tap_c, extent)
                pieces.append(
                    lax.dot_general(
                        flat_in, view, (((0,), (0,)), ((), ())), preferred_element_type=jnp.float32
                    )
                )
    return jnp.stack(pieces, axis=1)


def on_device(raw_weight, inputs, cotangent):
    extent = inputs.shape[:3]
    channels = inputs.shape[3]
    fan_count = channels * raw_weight.shape[1]
    padded = with_halo(cotangent, (("gx", 0), ("gy", 1), ("gz", 2)), 1)
    flat_in = inputs.reshape(-1, channels)
    sum_first, sum_second = lax.psum(
        (jnp.sum(raw_weight, axis=(0, 1)), jnp.sum(raw_weight * raw_weight, axis=(0, 1))),
        ("gx", "gy"),
    )
    mean_out = sum_first / fan_count
    var_out = sum_second / fan_count - mean_out * mean_out
    inv_std = lax.rsqrt(var_out + var_eps)
    std_float = (raw_weight - mean_out) * inv_std
    std_whole = lax.all_gather(std_float.astype(jnp.bfloat16), ("gx", "gy"), axis=0, tiled=True)
    input_grad = input_rows(padded, extent, std_whole)
    local_terms = filter_terms(padded, flat_in, extent)
    column_sum = lax.psum(local_terms, "gz")
    filter_grad = lax.psum_scatter(column_sum, ("gx", "gy"), scatter_dimension=0, tiled=True)
    local_grad = jnp.sum(filter_grad, axis=(0, 1))
    local_cross = jnp.sum(filter_grad * std_float, axis=(0, 1))
    local_square = jnp.sum(filter_grad * filter_grad, axis=(0, 1))
    sum_grad, sum_cross, sum_square = lax.psum(
        (local_grad, local_cross, local_square), ("gx", "gy")
    )
    mean_grad = sum_grad / fan_count
    mean_cross = sum_cross / fan_count
    raw_grad = inv_std * (filter_grad - mean_grad - std_float * mean_cross)
    per_output = sum_square - 2.0 * mean_grad * sum_grad - 2.0 * mean_cross * sum_cross
    per_output = (
        per_output
        + fan_count * mean_grad * mean_grad
        + fan_count * mean_cross * mean_cross * var_out / (var_out + var_eps)
    )
    square_sum = jnp.sum(inv_std * inv_std * per_output)
    scale = jnp.minimum(1.0, clip_norm * lax.rsqrt(square_sum + norm_eps))
    return (input_grad, raw_grad * scale)


def solution(mesh):
    in_specs = (P(("gx", "gy"), None, None), P("gx", "gy", "gz", None), P("gx", "gy", "gz", None))
    out_specs = (P("gx", "gy", "gz", None), P(("gx", "gy"), None, None))
    return jax.shard_map(
        on_device, mesh=mesh, in_specs=in_specs, out_specs=out_specs, check_vma=False
    )
```

profile of v0, /device:TPU:0, one launch (start us, length us, event | category | flops | bytes accessed | tf_op | source)
XLA Modules:
  0.0 215.6 jit_solution(4366381669883090917)
XLA Ops:
  8.2 2.4 %collective-permute-start = (bf16[1,16,16,128]{3,2,1,0:T(8,128)(2,1)S(1)}, bf16[1,16,16,128]{3,2,1,0:T(8,128)(2,1)S(1)}, u32[]{:S(2)}, u32[]{:S(2)}) collective-permute-start(bf16[1,16,16,128]{3,2,1,0:T(8,128)(2,1)S(1)} %get-tuple-element.51), channel_id=1, source_target_pairs={{0,16},{1,17},{2,18},{3,19},{4,20},{5,21},{6,22},{7,23},{8,24},{9,... | collective-permute-start | bytes 196616 | tf_op jit(solution)/shard_map/ppermute | solution.py:19
  10.6 1.3 collective-permute-start.1
  11.9 1.4 constant_dynamic-update-slice_fusion.5
  13.8 1.3 collective-permute-start.3
  15.1 4.8 %collective-permute-start.2 = (bf16[10,1,16,128]{3,2,1,0:T(8,128)(2,1)S(1)}, bf16[10,1,16,128]{3,2,1,0:T(8,128)(2,1)S(1)}, u32[]{:S(2)}, u32[]{:S(2)}) collective-permute-start(bf16[10,1,16,128]{3,2,1,0:T(8,128)(2,1)S(1)} %get-tuple-element.45), channel_id=1, source_target_pairs={{0,4},{4,8},{8,12},{1,5},{5,9},{9,13},{2,6},{6,10},{10,14},{3,7},{... | collective-permute-start | bytes 122888 | tf_op jit(solution)/shard_map/ppermute | solution.py:19
  20.3 1.3 collective-permute-done.2
  21.8 1.3 collective-permute-start.4
  23.1 4.6 %collective-permute-start.5 = (bf16[10,18,1,128]{3,2,1,0:T(2,128)(2,1)S(1)}, bf16[10,18,1,128]{3,2,1,0:T(2,128)(2,1)S(1)}, u32[]{:S(2)}, u32[]{:S(2)}) collective-permute-start(bf16[10,18,1,128]{3,2,1,0:T(2,128)(2,1)S(1)} %get-tuple-element.35), channel_id=1, source_target_pairs={{0,1},{1,2},{2,3},{4,5},{5,6},{6,7},{8,9},{9,10},{10,11},{12,13},{... | collective-permute-start | bytes 138248 | tf_op jit(solution)/shard_map/ppermute | solution.py:19
  28.3 1.5 collective-permute-done.5
  30.6 1.0 fusion.29
  31.6 1.0 fusion.10
  32.6 1.0 fusion.28
  33.5 1.0 fusion.27
  34.5 1.0 fusion.9
  35.5 1.0 fusion.26
  36.5 1.0 fusion.25
  37.4 1.0 fusion.8
  38.4 1.0 fusion.24
  39.4 1.0 fusion.23
  40.4 1.0 fusion.7
  42.3 1.0 fusion.21
  43.3 1.0 fusion.20
  44.3 1.0 fusion.19
  45.3 1.0 fusion.18
  46.3 1.0 fusion.6
  47.2 1.0 fusion.17
  48.2 1.0 fusion.16
  51.1 1.0 fusion.14
  52.1 1.0 fusion.4
  53.1 1.0 fusion.13
  54.1 1.0 fusion.12
  55.0 1.0 fusion.3
  56.0 1.0 fusion.11
  57.0 3.1 %copy.12 = f32[128,27,128]{2,1,0:T(8,128)} copy(f32[128,27,128]{0,2,1:T(8,128)} %fusion.11) | data formatting | bytes 3538944 | tf_op jit(solution)/shard_map/stack | solution.py:66
  60.2 1.0 multiply_reduce_fusion.2
  61.2 16.7 %all-reduce.1 = (f32[128]{0:T(128)S(1)}, f32[128]{0:T(128)S(1)}) all-reduce(f32[128]{0:T(128)S(1)} %get-tuple-element.8, f32[128]{0:T(128)S(1)} %get-tuple-element.7), channel_id=1, replica_groups=mesh['gx'=2,'gy'=4,'gz'=4] {'gx','gy'}, use_global_device_ids=true, to_apply=%region_1.0 | all-reduce | flops 256 | bytes 2048 | tf_op jit(solution)/shard_map/psum | solution.py:75
  77.9 1.9 slice.299
  79.8 1.9 slice.338
  81.7 1.7 fusion.32
  83.4 22.2 %reduce-scatter.2.cloned.1.call-done = f32[16,27,128]{2,1,0:T(8,128)} async-done(((f32[128,27,128]{2,1,0:T(8,128)}), f32[16,27,128]{2,1,0:T(8,128)}) %reduce-scatter.2.cloned.1.call-update) | async-done | bytes 221200 | tf_op jit(solution)/shard_map/reduce_scatter | solution.py:87
  105.6 1.8 copy.13
  107.4 3.7 %fusion.65 = (bf16[8,16,16,128]{3,2,1,0:T(8,128)(2,1)}, bf16[8,16,16,128]{3,2,1,0:T(8,128)(2,1)}, bf16[8,16,16,128]{3,2,1,0:T(8,128)(2,1)}, bf16[8,16,16,128]{3,...) fusion(bf16[10,18,17,128]{3,2,1,0:T(8,128)(2,1)S(1)} %get-tuple, ...), kind=kLoop, calls=%fused_computation.177 | loop fusion | bytes 18874368 | tf_op jit(solution)/shard_map/slice | solution.py:29
  111.1 32.5 %all-reduce.4.cloned.1.call-done = f32[16,27,128]{2,0,1:T(8,128)} async-done(((f32[16,27,128]{2,0,1:T(8,128)}), f32[16,27,128]{2,0,1:T(8,128)}) %all-reduce.4.cloned.1.call-update) | async-done | bytes 221200 | tf_op jit(solution)/shard_map/psum | solution.py:86
  143.6 1.1 multiply_reduce_fusion
  144.8 14.4 %all-reduce = (f32[128]{0:T(128)S(1)}, f32[128]{0:T(128)S(1)}, f32[128]{0:T(128)S(1)}) all-reduce(f32[128]{0:T(128)S(1)} %get-tuple-element.5, f32[128]{0:T(128)S(1)} %get-tuple-element.6, f32[128]{0:T(128)S(1)} %get-tuple-element.4), channel_id=1, replica_groups=mesh['gx'=2,'gy'=4,'gz'=4] {'gx','gy'}, use_global_device_ids=true, to_apply=%region_9.0 | all-reduce | flops 384 | bytes 3072 | tf_op jit(solution)/shard_map/psum | solution.py:91
  160.5 1.8 multiply_multiply_fusion
  162.3 27.9 %all_gather.3 = bf16[128,27,128]{2,0,1:T(8,128)(2,1)S(1)} all-gather(bf16[16,27,128]{2,0,1:T(8,128)(2,1)S(1)} %get-tuple-element.53), channel_id=1, replica_groups=mesh['gx'=2,'gy'=4,'gz'=4] {'gx','gy'}, dimensions={0}, use_global_device_ids=true | all-gather | bytes 995328 | tf_op jit(solution)/shard_map/all_gather | solution.py:83
  207.7 1.1 fusion.2
  (105 shorter events, 24.2 us)
Async XLA Ops:
  7.2 23.5 %copy-start = (bf16[8,16,16,128]{3,2,1,0:T(8,128)(2,1)S(1)}, bf16[8,16,16,128]{3,2,1,0:T(8,128)(2,1)}, u32[]{:S(2)}) copy-start(bf16[8,16,16,128]{3,2,1,0:T(8,128)(2,1)} %param.4) | copy-start | bytes 1572868
  7.2 98.4 %reduce-scatter.2.cloned.1.call-start = ((), (), s32[]{:S(2)}) async-start(), calls=%async_computation.1 | async-start | bytes 2359296 | tf_op jit(solution)/shard_map/reduce_scatter | solution.py:87
  8.2 3.7 %collective-permute-start = (bf16[1,16,16,128]{3,2,1,0:T(8,128)(2,1)S(1)}, bf16[1,16,16,128]{3,2,1,0:T(8,128)(2,1)S(1)}, u32[]{:S(2)}, u32[]{:S(2)}) collective-permute-start(bf16[1,16,16,128]{3,2,1,0:T(8,128)(2,1)S(1)} %get-tuple-element.51), channel_id=1, source_target_pairs={{0,16},{1,17},{2,18},{3,19},{4,20},{5,21},{6,22},{7,23},{8,24},{9,... | collective-permute-start | bytes 196616 | tf_op jit(solution)/shard_map/ppermute | solution.py:19
  10.6 3.1 %collective-permute-start.1 = (bf16[1,16,16,128]{3,2,1,0:T(8,128)(2,1)S(1)}, bf16[1,16,16,128]{3,2,1,0:T(8,128)(2,1)S(1)}, u32[]{:S(2)}, u32[]{:S(2)}) collective-permute-start(bf16[1,16,16,128]{3,2,1,0:T(8,128)(2,1)S(1)} %get-tuple-element.50), channel_id=1, source_target_pairs={{16,0},{17,1},{18,2},{19,3},{20,4},{21,5},{22,6},{23,7},{24,8},{25... | collective-permute-start | bytes 196616 | tf_op jit(solution)/shard_map/ppermute | solution.py:21
  13.3 38.8 %copy-start.29 = (bf16[9,16,16,128]{3,2,1,0:T(8,128)(2,1)}, bf16[9,16,16,128]{3,2,1,0:T(8,128)(2,1)S(1)}, u32[]{:S(2)}) copy-start(bf16[9,16,16,128]{3,2,1,0:T(8,128)(2,1)S(1)} %get-tuple-element.47) | copy-start | bytes 1769476
  13.7 20.8 %copy-start.28 = (bf16[9,16,16,128]{3,2,1,0:T(8,128)(2,1)}, bf16[9,16,16,128]{3,2,1,0:T(8,128)(2,1)S(1)}, u32[]{:S(2)}) copy-start(bf16[9,16,16,128]{3,2,1,0:T(8,128)(2,1)S(1)} %get-tuple-element.56) | copy-start | bytes 1769476
  13.8 6.6 %collective-permute-start.3 = (bf16[10,1,16,128]{3,2,1,0:T(8,128)(2,1)S(1)}, bf16[10,1,16,128]{3,2,1,0:T(8,128)(2,1)S(1)}, u32[]{:S(2)}, u32[]{:S(2)}) collective-permute-start(bf16[10,1,16,128]{3,2,1,0:T(8,128)(2,1)S(1)} %get-tuple-element.46), channel_id=1, source_target_pairs={{4,0},{8,4},{12,8},{5,1},{9,5},{13,9},{6,2},{10,6},{14,10},{7,3},{... | collective-permute-start | bytes 122888 | tf_op jit(solution)/shard_map/ppermute | solution.py:21
  15.1 6.6 %collective-permute-start.2 = (bf16[10,1,16,128]{3,2,1,0:T(8,128)(2,1)S(1)}, bf16[10,1,16,128]{3,2,1,0:T(8,128)(2,1)S(1)}, u32[]{:S(2)}, u32[]{:S(2)}) collective-permute-start(bf16[10,1,16,128]{3,2,1,0:T(8,128)(2,1)S(1)} %get-tuple-element.45), channel_id=1, source_target_pairs={{0,4},{4,8},{8,12},{1,5},{5,9},{9,13},{2,6},{6,10},{10,14},{3,7},{... | collective-permute-start | bytes 122888 | tf_op jit(solution)/shard_map/ppermute | solution.py:19
  21.8 6.5 %collective-permute-start.4 = (bf16[10,18,1,128]{3,2,1,0:T(2,128)(2,1)S(1)}, bf16[10,18,1,128]{3,2,1,0:T(2,128)(2,1)S(1)}, u32[]{:S(2)}, u32[]{:S(2)}) collective-permute-start(bf16[10,18,1,128]{3,2,1,0:T(2,128)(2,1)S(1)} %get-tuple-element.34), channel_id=1, source_target_pairs={{1,0},{2,1},{3,2},{5,4},{6,5},{7,6},{9,8},{10,9},{11,10},{13,12},{... | collective-permute-start | bytes 138248 | tf_op jit(solution)/shard_map/ppermute | solution.py:21
  23.1 6.7 %collective-permute-start.5 = (bf16[10,18,1,128]{3,2,1,0:T(2,128)(2,1)S(1)}, bf16[10,18,1,128]{3,2,1,0:T(2,128)(2,1)S(1)}, u32[]{:S(2)}, u32[]{:S(2)}) collective-permute-start(bf16[10,18,1,128]{3,2,1,0:T(2,128)(2,1)S(1)} %get-tuple-element.35), channel_id=1, source_target_pairs={{0,1},{1,2},{2,3},{4,5},{5,6},{6,7},{8,9},{9,10},{10,11},{12,13},{... | collective-permute-start | bytes 138248 | tf_op jit(solution)/shard_map/ppermute | solution.py:19
  42.3 1.0 copy-start.1
  60.2 83.5 %all-reduce.4.cloned.1.call-start = ((), (), s32[]{:S(2)}) async-start(), calls=%async_computation.2 | async-start | bytes 442368 | tf_op jit(solution)/shard_map/psum | solution.py:86
  144.8 45.7 %copy-start.22 = (bf16[8,16,16,128]{3,2,1,0:T(8,128)(2,1)S(1)}, bf16[8,16,16,128]{3,2,1,0:T(8,128)(2,1)}, u32[]{:S(2)}) copy-start(bf16[8,16,16,128]{3,2,1,0:T(8,128)(2,1)} %get-tuple-element.43) | copy-start | bytes 1572868
  190.1 1.0 copy-start.20
  190.4 1.1 copy-start.19
  191.5 1.1 copy-start.18
  191.8 1.1 copy-start.3
  192.9 1.0 copy-start.17
  193.2 1.1 copy-start.27
  194.2 1.1 copy-start.16
  194.6 1.1 copy-start.15
  195.6 1.1 copy-start.26
  196.0 1.1 copy-start.14
  197.0 1.1 copy-start.13
  197.4 1.1 copy-start.2
  198.3 1.1 copy-start.12
  198.7 1.1 copy-start.11
  199.7 1.1 copy-start.25
  200.1 1.1 copy-start.10
  201.1 1.1 copy-start.9
  201.5 1.1 copy-start.24
  202.4 1.1 copy-start.8
  202.9 1.1 copy-start.7
  203.8 1.1 copy-start.21
  204.3 1.1 copy-start.6
  205.2 1.1 copy-start.5
  205.6 1.1 copy-start.23
  206.6 1.1 copy-start.4
Sparse Core Ops, SparseCore 0:
  60.3 45.2 reduce-scatter.1
  108.5 35.0 all-reduce.3
where the time goes:
time: 217 us; the launch traced here: 216 us
  waiting for transfers between devices  59 us (27%)
  blocking collectives  58.9 us (27%)
  matrix products  35 us (16%)
  local copies, waits for them, and re-layouts  24.4 us (11%)
  starting transfers between devices  15.8 us (7%)
  between operations  15.2 us (7%)
  other arithmetic  7.2 us (3%)
    psum x1, waiting for transfers between devices, on_device(): column_sum = lax.psum(local_terms, 'gz')  32.5 us
    all_gather x1, blocking collectives, on_device(): lax.all_gather(std_float.astype(jnp.bfloat16), ('gx', 'gy'), axis=0, tile...  27.9 us
    dot_general x27, matrix products, filter_terms(): lax.dot_general(flat_in, view, (((0,), (0,)), ((), ())), preferred_elemen...  26.3 us
    reduce_scatter x1, waiting for transfers between devices, on_device(): lax.psum_scatter(column_sum, ('gx', 'gy'), scatter_dimension=0, tiled=True)  22.2 us
    psum x1, blocking collectives, on_device(): lax.psum((jnp.sum(raw_weight, axis=(0, 1)), jnp.sum(raw_weight * raw_weig...  16.7 us
    psum x1, blocking collectives, on_device(): lax.psum((local_grad, local_cross, local_square), ('gx', 'gy'))  14.4 us
    ppermute x3, starting transfers between devices, with_halo(): lax.ppermute(tail, axis, [(i, (i + 1) % count) for i in range(ends)])  11.8 us
    unnamed x61, local copies, waits for them, and re-layouts  9.64 us
  transfers between devices with their start and end apart: 8, of which 7 were waited for; matrix products, arithmetic and copies ran while one was open for 5% of the time, Pallas kernels for 0%

commit v1 on v0

--- a/solution.py
+++ b/solution.py
@@ -1,3 +1,4 @@
+import functools
 import jax
 import jax.numpy as jnp
 from jax import lax
@@ -6,6 +7,15 @@
 var_eps = 1e-05
 norm_eps = 1e-06
 clip_norm = 600.0
+
+
+def meet_forms(u_in, mesh_dim):
+    local_now = lax.all_gather(u_in, mesh_dim)
+    r1 = jnp.sum(local_now, 0)
+    return r1
+
+
+_test_pipes = functools.partial(meet_forms, mesh_dim="gz")
 
 
 def with_halo(cells, sides, width):
@@ -83,7 +93,7 @@
     std_whole = lax.all_gather(std_float.astype(jnp.bfloat16), ("gx", "gy"), axis=0, tiled=True)
     input_grad = input_rows(padded, extent, std_whole)
     local_terms = filter_terms(padded, flat_in, extent)
-    column_sum = lax.psum(local_terms, "gz")
+    column_sum = _test_pipes(local_terms)
     filter_grad = lax.psum_scatter(column_sum, ("gx", "gy"), scatter_dimension=0, tiled=True)
     local_grad = jnp.sum(filter_grad, axis=(0, 1))
     local_cross = jnp.sum(filter_grad * std_float, axis=(0, 1))

time: 217 us -> 323 us (1.49)
  waiting for transfers between devices: 59 us -> 152 us
  other arithmetic: 7.2 us -> 15.9 us
  local copies, waits for them, and re-layouts: 24.4 us -> 32 us
    all_gather x0 -> x1, waiting for transfers between devices: none -> 130 us  [meet_forms(): local_now = lax.all_gather(u_in, mesh_dim)]
    psum x1 -> x0, waiting for transfers between devices: 32.5 us -> none  [on_device(): column_sum = lax.psum(local_terms, 'gz')]
    reduce_sum x0 -> x2, other arithmetic: none -> 9.72 us  [the longest x1 8.56 us: meet_forms(): r1 = jnp.sum(local_now, 0)]
    all_gather x0 -> x1, local copies, waits for them, and re-layouts: none -> 9.14 us  [meet_forms(): local_now = lax.all_gather(u_in, mesh_dim)]
    reduce_scatter x1, waiting for transfers between devices: 22.2 us -> 15.1 us  [on_device(): lax.psum_scatter(column_sum, ('gx', 'gy'), scatter_dimension=0, tiled=True)]
    ppermute x3, waiting for transfers between devices: 1.4 us -> 5.15 us  [with_halo(): lax.ppermute(head, axis, [((i + 1) % count, i) for i in range(ends)])]
    unnamed x61 -> x63, local copies, waits for them, and re-layouts: 9.64 us -> 9.96 us
  transfers between devices with their start and end apart: 8 -> 8, of which waited for: 7 -> 7; matrix products, arithmetic and copies ran while one was open for 5% -> 3% of each run, Pallas kernels for 0% -> 0%
where the time goes in v1:
time: 323 us; the launch traced here: 322 us
  waiting for transfers between devices  152 us (47%)
  blocking collectives  56.5 us (17%)
  matrix products  34.8 us (11%)
  local copies, waits for them, and re-layouts  32 us (10%)
  other arithmetic  15.9 us (5%)
  starting transfers between devices  15.3 us (5%)
  between operations  15.2 us (5%)
    all_gather x1, waiting for transfers between devices, meet_forms(): local_now = lax.all_gather(u_in, mesh_dim)  130 us
    all_gather x1, blocking collectives, on_device(): lax.all_gather(std_float.astype(jnp.bfloat16), ('gx', 'gy'), axis=0, tile...  28 us
    dot_general x27, matrix products, filter_terms(): lax.dot_general(flat_in, view, (((0,), (0,)), ((), ())), preferred_elemen...  26.1 us
    reduce_scatter x1, waiting for transfers between devices, on_device(): lax.psum_scatter(column_sum, ('gx', 'gy'), scatter_dimension=0, tiled=True)  15.1 us
    psum x1, blocking collectives, on_device(): lax.psum((jnp.sum(raw_weight, axis=(0, 1)), jnp.sum(raw_weight * raw_weig...  14.3 us
    psum x1, blocking collectives, on_device(): lax.psum((local_grad, local_cross, local_square), ('gx', 'gy'))  14.2 us
    ppermute x3, starting transfers between devices, with_halo(): lax.ppermute(tail, axis, [(i, (i + 1) % count) for i in range(ends)])  11.2 us
    unnamed x63, local copies, waits for them, and re-layouts  9.96 us
  transfers between devices with their start and end apart: 8, of which 7 were waited for; matrix products, arithmetic and copies ran while one was open for 3% of the time, Pallas kernels for 0%

profile of v1, /device:TPU:0, one launch (start us, length us, event | category | flops | bytes accessed | tf_op | source)
XLA Modules:
  0.0 321.7 jit_solution(10586339014623994114)
XLA Ops:
  8.2 2.4 collective-permute-start
  10.6 1.3 collective-permute-start.1
  11.9 1.4 constant_dynamic-update-slice_fusion.5
  13.8 4.2 %collective-permute-start.2 = (bf16[10,1,16,128]{3,2,1,0:T(8,128)(2,1)S(1)}, bf16[10,1,16,128]{3,2,1,0:T(8,128)(2,1)S(1)}, u32[]{:S(2)}, u32[]{:S(2)}) collective-permute-start(bf16[10,1,16,128]{3,2,1,0:T(8,128)(2,1)S(1)} %get-tuple-element.44), channel_id=1, source_target_pairs={{0,4},{4,8},{8,12},{1,5},{5,9},{9,13},{2,6},{6,10},{10,14},{3,7},{... | collective-permute-start | bytes 122888 | tf_op jit(solution)/shard_map/ppermute | solution.py:29
  18.0 1.3 collective-permute-start.3
  19.7 4.2 %collective-permute-done.3 = bf16[10,1,16,128]{3,2,1,0:T(8,128)(2,1)S(1)} collective-permute-done((bf16[10,1,16,128]{3,2,1,0:T(8,128)(2,1)S(1)}, bf16[10,1,16,128]{3,2,1,0:T(8,128)(2,1)S(1)}, u32[]{:S(2)}, u32[]{:S(2)}) %collective-permute-start.3) | collective-permute-done | bytes 40992 | tf_op jit(solution)/shard_map/ppermute | solution.py:31
  24.0 1.3 collective-permute-start.4
  25.3 4.6 %collective-permute-start.5 = (bf16[10,18,1,128]{3,2,1,0:T(2,128)(2,1)S(1)}, bf16[10,18,1,128]{3,2,1,0:T(2,128)(2,1)S(1)}, u32[]{:S(2)}, u32[]{:S(2)}) collective-permute-start(bf16[10,18,1,128]{3,2,1,0:T(2,128)(2,1)S(1)} %get-tuple-element.34), channel_id=1, source_target_pairs={{0,1},{1,2},{2,3},{4,5},{5,6},{6,7},{8,9},{9,10},{10,11},{12,13},{... | collective-permute-start | bytes 138248 | tf_op jit(solution)/shard_map/ppermute | solution.py:29
  30.5 1.5 collective-permute-done.5
  32.9 1.0 fusion.29
  34.8 1.0 fusion.28
  35.8 1.0 fusion.27
  36.7 1.0 fusion.9
  37.7 1.0 fusion.26
  38.7 1.0 fusion.25
  40.6 1.0 fusion.24
  41.5 1.0 fusion.23
  42.5 1.0 fusion.7
  43.5 1.0 fusion.22
  44.5 1.0 fusion.21
  45.5 1.0 fusion.20
  46.5 1.0 fusion.19
  47.4 1.0 fusion.18
  48.4 1.0 fusion.6
  49.4 1.0 fusion.17
  50.3 1.0 fusion.16
  52.3 1.0 fusion.15
  53.2 1.0 fusion.14
  54.2 1.0 fusion.4
  55.2 1.0 fusion.13
  56.2 1.0 fusion.12
  58.1 1.0 fusion.11
  59.3 129.6 %all-gather.3.cloned.1.call-done = f32[512,27,128]{0,2,1:T(8,128)} async-done(((f32[128,27,128]{0,2,1:T(8,128)}), f32[512,27,128]{0,2,1:T(8,128)}) %all-gather.3.cloned.1.call-update) | async-done | bytes 7077904 | tf_op jit(solution)/shard_map/all_gather | solution.py:13
  188.9 9.1 %reshape.148 = f32[4,128,27,128]{1,0,3,2:T(4,128)} reshape(f32[512,27,128]{0,2,1:T(8,128)} %all-gather.3.cloned.1.call-done) | data formatting | bytes 14155776 | tf_op jit(solution)/shard_map/all_gather | solution.py:13
  198.1 8.6 %reduce_sum.65 = f32[128,27,128]{0,2,1:T(8,128)} reduce(f32[4,128,27,128]{1,0,3,2:T(4,128)} %reshape.148, f32[]{:T(128)} %constant.15.clone.1), dimensions={0}, to_apply=%region_4.0 | reduce | flops 1327104 | bytes 8847364 | tf_op jit(solution)/shard_map/reduce_sum | solution.py:14
  206.6 3.1 copy.14
  210.8 14.3 %all-reduce.1 = (f32[128]{0:T(128)S(1)}, f32[128]{0:T(128)S(1)}) all-reduce(f32[128]{0:T(128)S(1)} %get-tuple-element.7, f32[128]{0:T(128)S(1)} %get-tuple-element.6), channel_id=1, replica_groups=mesh['gx'=2,'gy'=4,'gz'=4] {'gx','gy'}, use_global_device_ids=true, to_apply=%region_1.0 | all-reduce | flops 256 | bytes 2048 | tf_op jit(solution)/shard_map/psum | solution.py:85
  225.1 1.9 slice.299
  227.0 1.9 slice.338
  228.8 1.7 fusion.32
  230.5 3.6 %fusion.65 = (bf16[8,16,16,128]{3,2,1,0:T(8,128)(2,1)S(1)}, bf16[8,16,16,128]{3,2,1,0:T(8,128)(2,1)}, bf16[8,16,16,128]{3,2,1,0:T(8,128)(2,1)}, bf16[8,16,16,128...) fusion(bf16[10,18,17,128]{3,2,1,0:T(8,128)(2,1)S(1)} %get-tuple, ...), kind=kLoop, calls=%fused_computation.177 | loop fusion | bytes 18874368 | tf_op jit(solution)/shard_map/slice | solution.py:39
  234.2 15.1 %reduce-scatter.2.cloned.1.call-done = f32[16,27,128]{2,1,0:T(8,128)} async-done(((f32[128,27,128]{2,1,0:T(8,128)}), f32[16,27,128]{2,1,0:T(8,128)}) %reduce-scatter.2.cloned.1.call-update) | async-done | bytes 221200 | tf_op jit(solution)/shard_map/reduce_scatter | solution.py:97
  249.2 1.0 multiply_reduce_fusion
  250.3 1.2 multiply_reduce_fusion.1
  251.4 14.2 %all-reduce = (f32[128]{0:T(128)S(1)}, f32[128]{0:T(128)S(1)}, f32[128]{0:T(128)S(1)}) all-reduce(f32[128]{0:T(128)S(1)} %multiply_reduce_fusion.1, f32[128]{0:T(128)S(1)} %get-tuple-element.5, f32[128]{0:T(128)S(1)} %get-tuple-element.4), channel_id=1, replica_groups=mesh['gx'=2,'gy'=4,'gz'=4] {'gx','gy'}, use_global_device_ids=true, to_apply=%region_9.0 | all-reduce | flops 384 | bytes 3072 | tf_op jit(solution)/shard_map/psum | solution.py:101
  267.0 1.9 multiply_multiply_fusion
  268.8 28.0 %all_gather.9 = bf16[128,27,128]{2,0,1:T(8,128)(2,1)S(1)} all-gather(bf16[16,27,128]{2,0,1:T(8,128)(2,1)S(1)} %get-tuple-element.52), channel_id=1, replica_groups=mesh['gx'=2,'gy'=4,'gz'=4] {'gx','gy'}, dimensions={0}, use_global_device_ids=true | all-gather | bytes 995328 | tf_op jit(solution)/shard_map/all_gather | solution.py:93
  313.8 1.1 fusion.2
  (109 shorter events, 25.7 us)
Async XLA Ops:
  7.2 25.7 %copy-start = (bf16[8,16,16,128]{3,2,1,0:T(8,128)(2,1)S(1)}, bf16[8,16,16,128]{3,2,1,0:T(8,128)(2,1)}, u32[]{:S(2)}) copy-start(bf16[8,16,16,128]{3,2,1,0:T(8,128)(2,1)} %param.4) | copy-start | bytes 1572868
  7.2 181.8 %all-gather.3.cloned.1.call-start = ((), (), s32[]{:S(2)}) async-start(), calls=%async_computation.2 | async-start | bytes 8847360 | tf_op jit(solution)/shard_map/all_gather | solution.py:13
  8.2 3.7 %collective-permute-start = (bf16[1,16,16,128]{3,2,1,0:T(8,128)(2,1)S(1)}, bf16[1,16,16,128]{3,2,1,0:T(8,128)(2,1)S(1)}, u32[]{:S(2)}, u32[]{:S(2)}) collective-permute-start(bf16[1,16,16,128]{3,2,1,0:T(8,128)(2,1)S(1)} %get-tuple-element.50), channel_id=1, source_target_pairs={{0,16},{1,17},{2,18},{3,19},{4,20},{5,21},{6,22},{7,23},{8,24},{9,... | collective-permute-start | bytes 196616 | tf_op jit(solution)/shard_map/ppermute | solution.py:29
  10.6 3.1 collective-permute-start.1
  13.3 40.9 %copy-start.30 = (bf16[9,16,16,128]{3,2,1,0:T(8,128)(2,1)}, bf16[9,16,16,128]{3,2,1,0:T(8,128)(2,1)S(1)}, u32[]{:S(2)}) copy-start(bf16[9,16,16,128]{3,2,1,0:T(8,128)(2,1)S(1)} %get-tuple-element.46) | copy-start | bytes 1769476
  13.7 23.0 %copy-start.29 = (bf16[9,16,16,128]{3,2,1,0:T(8,128)(2,1)}, bf16[9,16,16,128]{3,2,1,0:T(8,128)(2,1)S(1)}, u32[]{:S(2)}) copy-start(bf16[9,16,16,128]{3,2,1,0:T(8,128)(2,1)S(1)} %get-tuple-element.55) | copy-start | bytes 1769476
  13.8 5.9 %collective-permute-start.2 = (bf16[10,1,16,128]{3,2,1,0:T(8,128)(2,1)S(1)}, bf16[10,1,16,128]{3,2,1,0:T(8,128)(2,1)S(1)}, u32[]{:S(2)}, u32[]{:S(2)}) collective-permute-start(bf16[10,1,16,128]{3,2,1,0:T(8,128)(2,1)S(1)} %get-tuple-element.44), channel_id=1, source_target_pairs={{0,4},{4,8},{8,12},{1,5},{5,9},{9,13},{2,6},{6,10},{10,14},{3,7},{... | collective-permute-start | bytes 122888 | tf_op jit(solution)/shard_map/ppermute | solution.py:29
  18.0 5.9 %collective-permute-start.3 = (bf16[10,1,16,128]{3,2,1,0:T(8,128)(2,1)S(1)}, bf16[10,1,16,128]{3,2,1,0:T(8,128)(2,1)S(1)}, u32[]{:S(2)}, u32[]{:S(2)}) collective-permute-start(bf16[10,1,16,128]{3,2,1,0:T(8,128)(2,1)S(1)} %get-tuple-element.45), channel_id=1, source_target_pairs={{4,0},{8,4},{12,8},{5,1},{9,5},{13,9},{6,2},{10,6},{14,10},{7,3},{... | collective-permute-start | bytes 122888 | tf_op jit(solution)/shard_map/ppermute | solution.py:31
  24.0 6.4 %collective-permute-start.4 = (bf16[10,18,1,128]{3,2,1,0:T(2,128)(2,1)S(1)}, bf16[10,18,1,128]{3,2,1,0:T(2,128)(2,1)S(1)}, u32[]{:S(2)}, u32[]{:S(2)}) collective-permute-start(bf16[10,18,1,128]{3,2,1,0:T(2,128)(2,1)S(1)} %get-tuple-element.33), channel_id=1, source_target_pairs={{1,0},{2,1},{3,2},{5,4},{6,5},{7,6},{9,8},{10,9},{11,10},{13,12},{... | collective-permute-start | bytes 138248 | tf_op jit(solution)/shard_map/ppermute | solution.py:31
  25.3 6.7 %collective-permute-start.5 = (bf16[10,18,1,128]{3,2,1,0:T(2,128)(2,1)S(1)}, bf16[10,18,1,128]{3,2,1,0:T(2,128)(2,1)S(1)}, u32[]{:S(2)}, u32[]{:S(2)}) collective-permute-start(bf16[10,18,1,128]{3,2,1,0:T(2,128)(2,1)S(1)} %get-tuple-element.34), channel_id=1, source_target_pairs={{0,1},{1,2},{2,3},{4,5},{5,6},{6,7},{8,9},{9,10},{10,11},{12,13},{... | collective-permute-start | bytes 138248 | tf_op jit(solution)/shard_map/ppermute | solution.py:29
  44.5 1.0 copy-start.2
  59.1 190.1 %reduce-scatter.2.cloned.1.call-start = ((), (), s32[]{:S(2)}) async-start(), calls=%async_computation.1 | async-start | bytes 2359296 | tf_op jit(solution)/shard_map/reduce_scatter | solution.py:97
  209.8 0.9 copy-start.28
  234.1 62.7 %copy-start.22 = (bf16[8,16,16,128]{3,2,1,0:T(8,128)(2,1)S(1)}, bf16[8,16,16,128]{3,2,1,0:T(8,128)(2,1)}, u32[]{:S(2)}) copy-start(bf16[8,16,16,128]{3,2,1,0:T(8,128)(2,1)} %get-tuple-element.42) | copy-start | bytes 1572868
  296.9 1.0 copy-start.20
  297.2 1.1 copy-start.19
  298.2 1.1 copy-start.18
  298.5 1.1 copy-start.4
  299.6 1.0 copy-start.17
  299.9 1.1 copy-start.27
  301.0 1.1 copy-start.16
  301.3 1.1 copy-start.15
  302.3 1.1 copy-start.26
  302.7 1.1 copy-start.14
  303.7 1.1 copy-start.13
  304.1 1.1 copy-start.3
  305.0 1.1 copy-start.12
  305.5 1.1 copy-start.11
  306.4 1.1 copy-start.25
  306.8 1.1 copy-start.10
  307.8 1.1 copy-start.9
  308.2 1.1 copy-start.24
  309.2 1.1 copy-start.8
  309.6 1.1 copy-start.7
  310.5 1.1 copy-start.21
  311.0 1.1 copy-start.6
  311.9 1.1 copy-start.5
  312.4 1.1 copy-start.23
  313.3 1.6 copy-start.1
Sparse Core Ops, SparseCore 0:
  59.2 129.6 all-gather.2
  209.9 39.2 reduce-scatter.1
